TPU v7x, 32 devices: a whole 2x2x4 slice. The times are simulated.
32 devices in a mesh: py: 4 (over z), pz: 8 (over y, x, core).
Axes of the slice: x: 2, y: 2, z: 4, core: 2. Of those that a mesh axis runs over, the one named last changes fastest.
Arguments:
- field: bfloat16 [128, 128, 64, 256], P('py', 'pz'), may hold values from -60 to 60
- spectral_weights: bfloat16 [32, 32, 32, 2, 64, 64], P('py', 'pz'), may hold values from -0.5 to 0.5
- bypass_weight: bfloat16 [64, 64], replicated, may hold values from -0.75 to 0.75
Outputs:
- normalized: bfloat16 [128, 128, 64, 256], P('py', 'pz')
All inputs are finite; a program needn't handle non-finite values.
Results may differ from a plain program's by a relative error of at most 0.0081.
Values may be sent and summed in bfloat16 or wider, within the bound.
A program may use at most 192 MiB of HBM per device.

v0:
```python
import math
import jax
import jax.numpy as jnp
from jax import lax
from jax.sharding import PartitionSpec as P

NX = 256
NY = 128
NZ = 128
C = 64
MODES = 32


def mode_frequencies(mode_count):
    ordinal = jnp.arange(mode_count, dtype=jnp.float32)
    return jnp.where(ordinal < mode_count // 2, ordinal, ordinal - mode_count)


def phase_angles(length, mode_count):
    points = jnp.arange(length, dtype=jnp.float32)
    return 2.0 * math.pi / length * points[:, None] * mode_frequencies(mode_count)[None, :]


def real_forward(length, mode_count):
    angles = phase_angles(length, mode_count)
    matrix = jnp.stack([jnp.cos(angles), -jnp.sin(angles)], axis=2).reshape(length, 2 * mode_count)
    return (matrix / math.sqrt(length)).astype(jnp.bfloat16)


def complex_forward(length, mode_count):
    angles = phase_angles(length, mode_count)
    cosine = jnp.cos(angles)
    sine_part = jnp.sin(angles)
    from_real = jnp.stack([cosine, -sine_part], axis=2)
    from_imag = jnp.stack([sine_part, cosine], axis=2)
    return (jnp.stack([from_real, from_imag], axis=1) / math.sqrt(length)).astype(jnp.bfloat16)


def complex_inverse(length, mode_count):
    angles = phase_angles(length, mode_count).T
    cosine = jnp.cos(angles)
    sine_part = jnp.sin(angles)
    from_real = jnp.stack([cosine, sine_part], axis=2)
    from_imag = jnp.stack([-sine_part, cosine], axis=2)
    return (jnp.stack([from_real, from_imag], axis=1) / math.sqrt(mode_count)).astype(jnp.bfloat16)


def real_inverse(length, mode_count):
    angles = phase_angles(length, mode_count).T
    matrix = jnp.stack([jnp.cos(angles), -jnp.sin(angles)], axis=1).reshape(2 * mode_count, length)
    return (matrix / math.sqrt(mode_count)).astype(jnp.bfloat16)


def mix_modes(spectrum, weights):
    real_in = spectrum[..., 0]
    imag_in = spectrum[..., 1]
    real_w = weights[:, :, :, 0]
    imag_w = weights[:, :, :, 1]

    def product(operand, coefficient):
        return jnp.einsum(
            "cabk,abkco->oabk", operand, coefficient, preferred_element_type=jnp.float32
        )

    real_out = product(real_in, real_w) - product(imag_in, imag_w)
    imag_out = product(real_in, imag_w) + product(imag_in, real_w)
    return jnp.stack([real_out, imag_out], axis=-1).astype(jnp.bfloat16)


def on_device(field, spectral_weights, bypass_weight):
    row_table = real_forward(NX, MODES)
    forward_plane = complex_forward(NY, MODES)
    forward_column = complex_forward(NZ, MODES)
    inverse_column = complex_inverse(NZ, MODES)
    inverse_plane = complex_inverse(NY, MODES)
    inverse_row = real_inverse(NX, MODES)
    flat = jnp.dot(field.reshape(-1, NX), row_table, preferred_element_type=jnp.float32)
    row_modes = flat.reshape(field.shape[:3] + (2 * MODES,)).astype(jnp.bfloat16)
    incoming = lax.all_to_all(row_modes, "py", split_axis=3, concat_axis=0, tiled=True)
    paired = incoming.reshape(incoming.shape[:3] + (-1, 2))
    plane_modes = jnp.einsum(
        "yzcmp,ypkq->zcmkq", paired, forward_plane, preferred_element_type=jnp.float32
    ).astype(jnp.bfloat16)
    plane_modes = plane_modes.reshape(plane_modes.shape[:3] + (-1,))
    incoming = lax.all_to_all(plane_modes, "pz", split_axis=3, concat_axis=0, tiled=True)
    paired = incoming.reshape(incoming.shape[:3] + (-1, 2))
    spectrum = jnp.einsum(
        "zcakp,zpjq->cakjq", paired, forward_column, preferred_element_type=jnp.float32
    ).astype(jnp.bfloat16)
    mixed_modes = mix_modes(spectrum, spectral_weights)
    column_back = jnp.einsum(
        "oabkp,kpzq->zoabq", mixed_modes, inverse_column, preferred_element_type=jnp.float32
    ).astype(jnp.bfloat16)
    column_back = column_back.reshape(column_back.shape[:3] + (-1,))
    incoming = lax.all_to_all(column_back, "pz", split_axis=0, concat_axis=3, tiled=True)
    paired = incoming.reshape(incoming.shape[:3] + (-1, 2))
    plane_back = jnp.einsum(
        "zcakp,kpyq->yzcaq", paired, inverse_plane, preferred_element_type=jnp.float32
    ).astype(jnp.bfloat16)
    plane_back = plane_back.reshape(plane_back.shape[:3] + (-1,))
    incoming = lax.all_to_all(plane_back, "py", split_axis=0, concat_axis=3, tiled=True)
    points = jnp.dot(
        incoming.reshape(-1, 2 * MODES), inverse_row, preferred_element_type=jnp.float32
    )
    spectral = points.reshape(incoming.shape[:3] + (NX,))
    bypass = jnp.einsum("yzcx,co->yzox", field, bypass_weight, preferred_element_type=jnp.float32)
    activated = jax.nn.gelu(spectral + bypass, approximate=True)
    entries = NX * NY * NZ * C
    summed, squared = lax.psum((jnp.sum(activated), jnp.sum(activated * activated)), ("py", "pz"))
    field_mean = summed / entries
    field_var = squared / entries - field_mean * field_mean
    return ((activated - field_mean) * lax.rsqrt(field_var + 1e-05)).astype(jnp.bfloat16)


def solution(mesh):
    in_specs = (P("py", "pz", None, None), P("py", "pz", None, None, None, None), P())
    out_specs = P("py", "pz", None, None)
    return jax.shard_map(
        on_device, mesh=mesh, in_specs=in_specs, out_specs=out_specs, check_vma=False
    )
```

profile of v0, /device:TPU:12, one launch (start us, length us, event | category | flops | bytes accessed | tf_op | source)
XLA Modules:
  0.0 524.4 jit_solution(14442338689824171746)
XLA Ops:
  0.3 12.8 %fusion = bf16[32768,64]{0,1:T(8,128)(2,1)} fusion(bf16[256,64]{0,1:T(8,128)(2,1)S(1)} %convert_element_type.65, bf16[32768,256]{1,0:T(8,128)(2,1)} %bitcast.144), kind=kOutput, calls=%fused_computation.2 | convolution fusion | flops 1075838976 | bytes 21004288 | tf_op jit(solution)/shard_map/dot_general | solution.py:77
  13.2 11.3 %convert_element_type.68 = bf16[32,16,64,64]{2,1,0,3:T(8,128)(2,1)} reshape(bf16[32768,64]{0,1:T(8,128)(2,1)} %fusion) | data formatting | bytes 8388608 | tf_op jit(solution)/shard_map/convert_element_type | solution.py:78
  24.5 9.5 %reshape.532 = bf16[4,2,262144]{2,1,0:T(2,128)(2,1)} reshape(bf16[64,32,16,64]{3,2,1,0:T(8,128)(2,1)} %bitcast.145) | data formatting | bytes 8388608
  40.0 89.9 %all-to-all-done = bf16[4,2,262144]{2,1,0:T(2,128)(2,1)} async-done(((bf16[4,2,262144]{2,1,0:T(2,128)(2,1)}), bf16[4,2,262144]{2,1,0:T(2,128)(2,1)}, u32[]{:S(2)}, u32[]{:S(2)}) %all-to-all-start) | async-done | bytes 4194336 | tf_op jit(solution)/shard_map/all_to_all | solution.py:79
  129.9 9.3 %reshape.533 = bf16[64,32,16,64]{3,2,1,0:T(8,128)(2,1)} reshape(bf16[4,2,262144]{2,1,0:T(2,128)(2,1)} %all-to-all-done) | data formatting | bytes 8388608
  139.1 9.0 %copy.102 = bf16[4,32,16,64,16]{3,2,4,1,0:T(8,128)(2,1)} copy(bf16[4,32,16,64,16]{3,2,1,4,0:T(8,128)(2,1)} %bitcast.147) | data formatting | bytes 8388608 | tf_op jit(solution)/shard_map/all_to_all | solution.py:79
  148.2 13.8 %copy.120 = bf16[128,16,64,8,2,1]{0,3,4,5,2,1:T(8,128)(2,1)} copy(bf16[128,16,64,8,2,1]{2,1,4,3,0,5:T(8,128)(2,1)} %bitcast.148) | data formatting | bytes 8388608 | tf_op jit(solution)/shard_map/reshape | solution.py:80
  167.3 6.0 %copy.140 = bf16[16,64,8,32,2]{1,2,0,4,3:T(8,128)(2,1)S(1)} copy(bf16[16,64,8,32,2]{3,2,4,1,0:T(8,128)(2,1)} %bitcast_convert_fusion.1) | data formatting | bytes 2097152 | tf_op jit(solution)/shard_map/reshape | solution.py:84
  180.6 13.7 %all-to-all-done.1 = bf16[8,2,32768]{2,1,0:T(2,128)(2,1)S(1)} async-done(((bf16[8,2,32768]{2,1,0:T(2,128)(2,1)}), bf16[8,2,32768]{2,1,0:T(2,128)(2,1)S(1)}, u32[]{:S(2)}, u32[]{:S(2)}) %all-to-all-start.1) | async-done | bytes 1048608 | tf_op jit(solution)/shard_map/all_to_all | solution.py:85
  203.5 8.1 %fusion.8 = f32[8,4,32,1,64]{4,3,2,1,0:T(1,128)S(1)} fusion(bf16[64,8,4,32,1]{0,4,3,2,1:T(2,128)(2,1)S(1)} %copy.125, bf16[8,4,32,2,64,64]{5,4,3,2,1,0:T(8,128)(2,1)} %param.4), kind=kOutput, calls=%fused_computation.13 | convolution fusion | flops 8388608 | bytes 17170432 | tf_op jit(solution)/shard_map/cabk,abkco->oabk/dot_general | solution.py:61
  211.6 8.1 %fusion.14 = f32[8,4,32,1,64]{4,3,2,1,0:T(1,128)S(1)} fusion(bf16[64,8,4,32,1]{0,4,3,2,1:T(2,128)(2,1)S(1)} %copy.125, bf16[8,4,32,2,64,64]{5,4,3,2,1,0:T(8,128)(2,1)} %param.4), kind=kOutput, calls=%fused_computation.19 | convolution fusion | flops 8388608 | bytes 17170432 | tf_op jit(solution)/shard_map/cabk,abkco->oabk/dot_general | solution.py:61
  220.4 8.1 %fusion.12 = f32[8,4,32,1,64]{4,3,2,1,0:T(1,128)S(1)} fusion(bf16[64,8,4,32,1]{0,4,3,2,1:T(2,128)(2,1)S(1)} %copy.127, bf16[8,4,32,2,64,64]{5,4,3,2,1,0:T(8,128)(2,1)} %param.4), kind=kOutput, calls=%fused_computation.17 | convolution fusion | flops 8388608 | bytes 17170432 | tf_op jit(solution)/shard_map/cabk,abkco->oabk/dot_general | solution.py:61
  228.5 8.3 %fusion.10 = f32[8,4,32,1,64]{4,3,2,1,0:T(1,128)S(1)} fusion(bf16[64,8,4,32,1]{0,4,3,2,1:T(2,128)(2,1)S(1)} %copy.127, bf16[8,4,32,2,64,64]{5,4,3,2,1,0:T(8,128)(2,1)} %param.4), kind=kOutput, calls=%fused_computation.15 | convolution fusion | flops 8388608 | bytes 17170432 | tf_op jit(solution)/shard_map/cabk,abkco->oabk/dot_general | solution.py:61
  243.4 18.4 %all_to_all.60 = bf16[8,2,32768]{2,1,0:T(2,128)(2,1)} all-to-all(bf16[8,2,32768]{2,1,0:T(2,128)(2,1)S(1)} %reshape.536), channel_id=1, replica_groups=mesh['py'=4,'pz'=8] {'pz'}, dimensions={0} | all-to-all | bytes 2097152 | tf_op jit(solution)/shard_map/all_to_all | solution.py:95
  269.8 12.8 %copy.115 = bf16[128,16,64,16]{2,3,1,0:T(8,128)(2,1)} copy(bf16[128,16,64,16]{0,2,3,1:T(8,128)(2,1)} %bitcast.150) | data formatting | bytes 8388608 | tf_op jit(solution)/shard_map/reshape | solution.py:100
  282.6 9.5 %reshape.538 = bf16[4,2,262144]{2,1,0:T(2,128)(2,1)} reshape(bf16[128,16,16,64]{3,2,1,0:T(8,128)(2,1)} %bitcast.146) | data formatting | bytes 8388608
  292.2 8.4 %all-to-all-start.3 = ((bf16[4,2,262144]{2,1,0:T(2,128)(2,1)}), bf16[4,2,262144]{2,1,0:T(2,128)(2,1)}, u32[]{:S(2)}, u32[]{:S(2)}) async-start(bf16[4,2,262144]{2,1,0:T(2,128)(2,1)} %reshape.538), calls=%async_computation.3 | async-start | bytes 8388608 | tf_op jit(solution)/shard_map/all_to_all | solution.py:101
  300.9 89.3 %all-to-all-done.3 = bf16[4,2,262144]{2,1,0:T(2,128)(2,1)} async-done(((bf16[4,2,262144]{2,1,0:T(2,128)(2,1)}), bf16[4,2,262144]{2,1,0:T(2,128)(2,1)}, u32[]{:S(2)}, u32[]{:S(2)}) %all-to-all-start.3) | async-done | bytes 4194336 | tf_op jit(solution)/shard_map/all_to_all | solution.py:101
  390.2 9.3 %reshape.539 = bf16[128,16,16,64]{3,2,1,0:T(8,128)(2,1)} reshape(bf16[4,2,262144]{2,1,0:T(2,128)(2,1)} %all-to-all-done.3) | data formatting | bytes 8388608
  399.4 9.0 %copy.116 = bf16[32,16,64,4,16]{2,4,3,1,0:T(8,128)(2,1)} copy(bf16[32,16,64,4,16]{2,4,1,0,3:T(8,128)(2,1)} %bitcast.149) | data formatting | bytes 8388608 | tf_op jit(solution)/shard_map/all_to_all | solution.py:101
  408.5 19.0 %fusion.36 = f32[32,16,64,256]{3,2,1,0:T(8,128)} fusion(bf16[32,16,64,64]{2,3,1,0:T(8,128)(2,1)} %bitcast.143, bf16[64,256,1,1]{1,0,2,3:T(8,128)(2,1)S(1)} %reshape.529), kind=kOutput, calls=%fused_computation.62 | convolution fusion | flops 1073741824 | bytes 37781504 | tf_op jit(solution)/shard_map/dot_general | solution.py:102
  427.5 32.3 %fusion.54 = (f32[]{:T(128)}, f32[]{:T(128)}, f32[32,16,64,256]{3,2,1,0:T(8,128)}) fusion(f32[32,16,64,256]{3,2,1,0:T(8,128)} %fusion.36, bf16[32,16,64,256]{3,2,1,0:T(8,128)(2,1)} %param.3, bf16[64,64]{1,0:T(8,128)(2,1)S(1)} %copy-done), kind=kOutput, calls=%fused_computation.83 | convolution fusion | flops 1174405120 | bytes 83894280 | tf_op jit(solution)/shard_map/yzcx,co->yzox/dot_general | solution.py:106
  459.8 43.2 %all-reduce = (f32[]{:T(128)}, f32[]{:T(128)}) all-reduce(f32[]{:T(128)} %get-tuple-element.6, f32[]{:T(128)} %get-tuple-element.5), channel_id=1, replica_groups=mesh['py'=4,'pz'=8] {'py','pz'}, use_global_device_ids=true, to_apply=%region_3.4 | all-reduce | flops 2 | bytes 16 | tf_op jit(solution)/shard_map/psum | solution.py:109
  505.5 18.5 %multiply_convert_fusion = bf16[32,16,64,256]{3,2,1,0:T(8,128)(2,1)} fusion(f32[32,16,64,256]{3,2,1,0:T(8,128)} %get-tuple-element.25, f32[]{:T(128)S(6)} %rsqrt.3, f32[]{:T(128)S(6)} %div.32), kind=kLoop, calls=%fused_computation.11 | loop fusion | flops 25165824 | bytes 50331656 | tf_op jit(solution)/shard_map/convert_element_type | solution.py:112
  (37 shorter events, 43.4 us)
Async XLA Ops:
  0.0 427.5 %copy-start = (bf16[64,64]{1,0:T(8,128)(2,1)S(1)}, bf16[64,64]{1,0:T(8,128)(2,1)}, u32[]{:S(2)}) copy-start(bf16[64,64]{1,0:T(8,128)(2,1)} %param.5) | copy-start | bytes 24580
  34.0 95.8 %all-to-all-start = ((bf16[4,2,262144]{2,1,0:T(2,128)(2,1)}), bf16[4,2,262144]{2,1,0:T(2,128)(2,1)}, u32[]{:S(2)}, u32[]{:S(2)}) async-start(bf16[4,2,262144]{2,1,0:T(2,128)(2,1)} %reshape.532), calls=%async_computation | async-start | bytes 8388608 | tf_op jit(solution)/shard_map/all_to_all | solution.py:79
  176.0 18.3 %all-to-all-start.1 = ((bf16[8,2,32768]{2,1,0:T(2,128)(2,1)}), bf16[8,2,32768]{2,1,0:T(2,128)(2,1)S(1)}, u32[]{:S(2)}, u32[]{:S(2)}) async-start(bf16[8,2,32768]{2,1,0:T(2,128)(2,1)} %reshape.534), calls=%async_computation.1 | async-start | bytes 2097152 | tf_op jit(solution)/shard_map/all_to_all | solution.py:85
  292.2 98.0 %all-to-all-start.3 = ((bf16[4,2,262144]{2,1,0:T(2,128)(2,1)}), bf16[4,2,262144]{2,1,0:T(2,128)(2,1)}, u32[]{:S(2)}, u32[]{:S(2)}) async-start(bf16[4,2,262144]{2,1,0:T(2,128)(2,1)} %reshape.538), calls=%async_computation.3 | async-start | bytes 8388608 | tf_op jit(solution)/shard_map/all_to_all | solution.py:101
where the time goes:
time: 531 us; the launch traced here: 524 us
  waiting for transfers between devices  193 us (36%)
  local copies, waits for them, and re-layouts  124 us (23%)
  matrix products  104 us (20%)
  blocking collectives  61.6 us (12%)
  other arithmetic  19.5 us (4%)
  starting transfers between devices  18.7 us (4%)
    all_to_all x1, waiting for transfers between devices, on_device(): lax.all_to_all(row_modes, 'py', split_axis=3, concat_axis=0, tiled=True)  89.9 us
    all_to_all x1, waiting for transfers between devices, on_device(): lax.all_to_all(plane_back, 'py', split_axis=0, concat_axis=3, tiled=True)  89.3 us
    unnamed x10, local copies, waits for them, and re-layouts  46.5 us
    psum x1, blocking collectives, on_device(): lax.psum((jnp.sum(activated), jnp.sum(activated * activated)), ('py', 'pz'))  43.2 us
    dot_general x4, matrix products, product(): jnp.einsum('cabk,abkco->oabk', operand, coefficient, preferred_element_ty...  32.6 us
    dot_general x1, matrix products, on_device(): jnp.einsum('yzcx,co->yzox', field, bypass_weight, preferred_element_type=...  32.3 us
    dot_general x1, matrix products, on_device(): jnp.dot(incoming.reshape(-1, 2 * MODES), inverse_row, preferred_element_t...  19 us
    convert_element_type x1, other arithmetic, on_device(): ((activated - field_mean) * lax.rsqrt(field_var + 1e-05)).astype(jnp.bflo...  18.5 us
  transfers between devices with their start and end apart: 3, of which 3 were waited for; matrix products, arithmetic and copies ran while one was open for 0% of the time, Pallas kernels for 0%

commit v1 on v0

--- a/solution.py
+++ b/solution.py
@@ -98,7 +98,10 @@
         "zcakp,kpyq->yzcaq", paired, inverse_plane, preferred_element_type=jnp.float32
     ).astype(jnp.bfloat16)
     plane_back = plane_back.reshape(plane_back.shape[:3] + (-1,))
-    incoming = lax.all_to_all(plane_back, "py", split_axis=0, concat_axis=3, tiled=True)
+    incoming = jnp.concatenate(
+        lax.all_to_all(jnp.stack(jnp.split(plane_back, lax.axis_size("py"), axis=0)), "py", 0, 0),
+        axis=3,
+    )
     points = jnp.dot(
         incoming.reshape(-1, 2 * MODES), inverse_row, preferred_element_type=jnp.float32
     )

time: 531 us -> 563 us (1.060)
  local copies, waits for them, and re-layouts: 124 us -> 149 us
  other arithmetic: 19.5 us -> 26.7 us
    split x0 -> x5, local copies, waits for them, and re-layouts: none -> 31.3 us  [on_device(): jnp.split(plane_back, lax.axis_size('py'), axis=0)]
    all_to_all x1 -> x0, local copies, waits for them, and re-layouts: 9.03 us -> none  [on_device(): lax.all_to_all(plane_back, 'py', split_axis=0, concat_axis=3, tiled=True)]
    unnamed x0 -> x1, other arithmetic: none -> 7.2 us
    reshape x1 -> x2, local copies, waits for them, and re-layouts: 12.8 us -> 18.7 us  [on_device(): jnp.concatenate(lax.all_to_all(jnp.stack(jnp.split(plane_back, lax.axis_s...]
where the time goes in v1:
time: 563 us; the launch traced here: 557 us
  waiting for transfers between devices  193 us (34%)
  local copies, waits for them, and re-layouts  149 us (26%)
  matrix products  105 us (19%)
  blocking collectives  61.6 us (11%)
  other arithmetic  26.7 us (5%)
  starting transfers between devices  18.3 us (3%)
    all_to_all x1, waiting for transfers between devices, on_device(): lax.all_to_all(row_modes, 'py', split_axis=3, concat_axis=0, tiled=True)  89.9 us
    all_to_all x1, waiting for transfers between devices, on_device(): lax.all_to_all(jnp.stack(jnp.split(plane_back, lax.axis_size('py'), axis=...  89.3 us
    unnamed x10, local copies, waits for them, and re-layouts  46.5 us
    psum x1, blocking collectives, on_device(): lax.psum((jnp.sum(activated), jnp.sum(activated * activated)), ('py', 'pz'))  43.2 us
    dot_general x4, matrix products, product(): jnp.einsum('cabk,abkco->oabk', operand, coefficient, preferred_element_ty...  32.8 us
    dot_general x1, matrix products, on_device(): jnp.einsum('yzcx,co->yzox', field, bypass_weight, preferred_element_type=...  32.5 us
    split x5, local copies, waits for them, and re-layouts, on_device(): jnp.split(plane_back, lax.axis_size('py'), axis=0)  31.3 us
    dot_general x1, matrix products, on_device(): jnp.dot(incoming.reshape(-1, 2 * MODES), inverse_row, preferred_element_t...  19 us
  transfers between devices with their start and end apart: 3, of which 3 were waited for; matrix products, arithmetic and copies ran while one was open for 0% of the time, Pallas kernels for 0%

profile of v1, /device:TPU:12, one launch (start us, length us, event | category | flops | bytes accessed | tf_op | source)
XLA Modules:
  0.0 556.8 jit_solution(14066024160221188082)
XLA Ops:
  0.3 12.9 %fusion = bf16[32768,64]{0,1:T(8,128)(2,1)} fusion(bf16[256,64]{0,1:T(8,128)(2,1)S(1)} %convert_element_type.65, bf16[32768,256]{1,0:T(8,128)(2,1)} %bitcast.148), kind=kOutput, calls=%fused_computation.2 | convolution fusion | flops 1075838976 | bytes 21004288 | tf_op jit(solution)/shard_map/dot_general | solution.py:77
  13.2 11.3 %convert_element_type.68 = bf16[32,16,64,64]{2,1,0,3:T(8,128)(2,1)} reshape(bf16[32768,64]{0,1:T(8,128)(2,1)} %fusion) | data formatting | bytes 8388608 | tf_op jit(solution)/shard_map/convert_element_type | solution.py:78
  24.5 9.5 %reshape.539 = bf16[4,2,262144]{2,1,0:T(2,128)(2,1)} reshape(bf16[64,32,16,64]{3,2,1,0:T(8,128)(2,1)} %bitcast.149) | data formatting | bytes 8388608
  39.7 89.9 %all-to-all-done = bf16[4,2,262144]{2,1,0:T(2,128)(2,1)} async-done(((bf16[4,2,262144]{2,1,0:T(2,128)(2,1)}), bf16[4,2,262144]{2,1,0:T(2,128)(2,1)}, u32[]{:S(2)}, u32[]{:S(2)}) %all-to-all-start) | async-done | bytes 4194336 | tf_op jit(solution)/shard_map/all_to_all | solution.py:79
  129.6 9.3 %reshape.540 = bf16[64,32,16,64]{3,2,1,0:T(8,128)(2,1)} reshape(bf16[4,2,262144]{2,1,0:T(2,128)(2,1)} %all-to-all-done) | data formatting | bytes 8388608
  138.8 9.0 %copy.112 = bf16[4,32,16,64,16]{3,2,4,1,0:T(8,128)(2,1)} copy(bf16[4,32,16,64,16]{3,2,1,4,0:T(8,128)(2,1)} %bitcast.150) | data formatting | bytes 8388608 | tf_op jit(solution)/shard_map/all_to_all | solution.py:79
  147.9 13.8 %copy.132 = bf16[128,16,64,8,2,1]{0,3,4,5,2,1:T(8,128)(2,1)} copy(bf16[128,16,64,8,2,1]{2,1,4,3,0,5:T(8,128)(2,1)} %bitcast.151) | data formatting | bytes 8388608 | tf_op jit(solution)/shard_map/reshape | solution.py:80
  180.4 13.7 %all-to-all-done.1 = bf16[8,2,32768]{2,1,0:T(2,128)(2,1)S(1)} async-done(((bf16[8,2,32768]{2,1,0:T(2,128)(2,1)}), bf16[8,2,32768]{2,1,0:T(2,128)(2,1)S(1)}, u32[]{:S(2)}, u32[]{:S(2)}) %all-to-all-start.1) | async-done | bytes 1048608 | tf_op jit(solution)/shard_map/all_to_all | solution.py:85
  203.2 8.1 %fusion.8 = f32[8,4,32,1,64]{4,3,2,1,0:T(1,128)S(1)} fusion(bf16[64,8,4,32,1]{0,4,3,2,1:T(2,128)(2,1)S(1)} %copy.137, bf16[8,4,32,2,64,64]{5,4,3,2,1,0:T(8,128)(2,1)} %param.4), kind=kOutput, calls=%fused_computation.13 | convolution fusion | flops 8388608 | bytes 17170432 | tf_op jit(solution)/shard_map/cabk,abkco->oabk/dot_general | solution.py:61
  211.3 8.1 %fusion.14 = f32[8,4,32,1,64]{4,3,2,1,0:T(1,128)S(1)} fusion(bf16[64,8,4,32,1]{0,4,3,2,1:T(2,128)(2,1)S(1)} %copy.137, bf16[8,4,32,2,64,64]{5,4,3,2,1,0:T(8,128)(2,1)} %param.4), kind=kOutput, calls=%fused_computation.19 | convolution fusion | flops 8388608 | bytes 17170432 | tf_op jit(solution)/shard_map/cabk,abkco->oabk/dot_general | solution.py:61
  220.1 8.1 %fusion.12 = f32[8,4,32,1,64]{4,3,2,1,0:T(1,128)S(1)} fusion(bf16[64,8,4,32,1]{0,4,3,2,1:T(2,128)(2,1)S(1)} %copy.139, bf16[8,4,32,2,64,64]{5,4,3,2,1,0:T(8,128)(2,1)} %param.4), kind=kOutput, calls=%fused_computation.17 | convolution fusion | flops 8388608 | bytes 17170432 | tf_op jit(solution)/shard_map/cabk,abkco->oabk/dot_general | solution.py:61
  228.2 8.5 %fusion.10 = f32[8,4,32,1,64]{4,3,2,1,0:T(1,128)S(1)} fusion(bf16[64,8,4,32,1]{0,4,3,2,1:T(2,128)(2,1)S(1)} %copy.139, bf16[8,4,32,2,64,64]{5,4,3,2,1,0:T(8,128)(2,1)} %param.4), kind=kOutput, calls=%fused_computation.15 | convolution fusion | flops 8388608 | bytes 17170432 | tf_op jit(solution)/shard_map/cabk,abkco->oabk/dot_general | solution.py:61
  243.3 18.4 %all_to_all.50 = bf16[8,2,32768]{2,1,0:T(2,128)(2,1)} all-to-all(bf16[8,2,32768]{2,1,0:T(2,128)(2,1)S(1)} %reshape.543), channel_id=1, replica_groups=mesh['py'=4,'pz'=8] {'pz'}, dimensions={0} | all-to-all | bytes 2097152 | tf_op jit(solution)/shard_map/all_to_all | solution.py:95
  266.8 7.8 %fusion.55 = (bf16[32,16,64,8,2]{0,2,3,1,4:T(8,128)(2,1)}, bf16[32,16,64,8,2]{0,2,3,1,4:T(8,128)(2,1)}, bf16[32,16,64,8,2]{0,2,3,1,4:T(8,128)(2,1)}, bf16[32,16,64,8,2]{0,2,3,1,4:T(8,128)(2,1)}) fusion(bf16[128,16,64,8,2]{0,2,3,1,4:T(8,128)(2,1)S(1)} %fusion.20), kind=kLoop, calls=%fused_computation.85 | loop fusion | bytes 8388608 | tf_op jit(solution)/shard_map/split | solution.py:102
  305.3 9.5 %reshape.545 = bf16[4,2,262144]{2,1,0:T(2,128)(2,1)} reshape(bf16[4,32,16,16,64]{4,3,2,1,0:T(8,128)(2,1)} %fusion.56) | data formatting | bytes 8388608
  314.9 8.4 %all-to-all-start.3 = ((bf16[4,2,262144]{2,1,0:T(2,128)(2,1)}), bf16[4,2,262144]{2,1,0:T(2,128)(2,1)}, u32[]{:S(2)}, u32[]{:S(2)}) async-start(bf16[4,2,262144]{2,1,0:T(2,128)(2,1)} %reshape.545), calls=%async_computation.3 | async-start | bytes 8388608 | tf_op jit(solution)/shard_map/all_to_all | solution.py:102
  323.5 89.3 %all-to-all-done.3 = bf16[4,2,262144]{2,1,0:T(2,128)(2,1)} async-done(((bf16[4,2,262144]{2,1,0:T(2,128)(2,1)}), bf16[4,2,262144]{2,1,0:T(2,128)(2,1)}, u32[]{:S(2)}, u32[]{:S(2)}) %all-to-all-start.3) | async-done | bytes 4194336 | tf_op jit(solution)/shard_map/all_to_all | solution.py:102
  412.8 9.3 %reshape.546 = bf16[4,32,16,16,64]{4,3,2,1,0:T(8,128)(2,1)} reshape(bf16[4,2,262144]{2,1,0:T(2,128)(2,1)} %all-to-all-done.3) | data formatting | bytes 8388608
  422.1 9.9 %bitcast_bitcast_fusion = bf16[32,16,64,4,16]{2,1,4,0,3:T(8,128)(2,1)} fusion(bf16[4,32,16,16,64]{4,3,2,1,0:T(8,128)(2,1)} %reshape.546), kind=kLoop, calls=%fused_computation.86 | loop fusion | bytes 8388608 | tf_op jit(solution)/shard_map/reshape | solution.py:101
  432.0 8.7 %copy.128 = bf16[32,16,64,4,16]{2,4,3,1,0:T(8,128)(2,1)} copy(bf16[32,16,64,4,16]{2,1,4,0,3:T(8,128)(2,1)} %bitcast_bitcast_fusion) | data formatting | bytes 8388608 | tf_op jit(solution)/shard_map/reshape | solution.py:101
  440.7 19.0 %fusion.36 = f32[32,16,64,256]{3,2,1,0:T(8,128)} fusion(bf16[32,16,64,64]{2,3,1,0:T(8,128)(2,1)} %bitcast.147, bf16[64,256,1,1]{1,0,2,3:T(8,128)(2,1)S(1)} %reshape.536), kind=kOutput, calls=%fused_computation.63 | convolution fusion | flops 1073741824 | bytes 37781504 | tf_op jit(solution)/shard_map/dot_general | solution.py:105
  459.7 32.5 %fusion.54 = (f32[]{:T(128)}, f32[]{:T(128)}, f32[32,16,64,256]{3,2,1,0:T(8,128)}) fusion(f32[32,16,64,256]{3,2,1,0:T(8,128)} %fusion.36, bf16[32,16,64,256]{3,2,1,0:T(8,128)(2,1)} %param.3, bf16[64,64]{1,0:T(8,128)(2,1)S(1)} %copy-done), kind=kOutput, calls=%fused_computation.84 | convolution fusion | flops 1174405120 | bytes 83894280 | tf_op jit(solution)/shard_map/yzcx,co->yzox/dot_general | solution.py:109
  492.3 43.2 %all-reduce = (f32[]{:T(128)}, f32[]{:T(128)}) all-reduce(f32[]{:T(128)} %get-tuple-element.6, f32[]{:T(128)} %get-tuple-element.5), channel_id=1, replica_groups=mesh['py'=4,'pz'=8] {'py','pz'}, use_global_device_ids=true, to_apply=%region_3.4 | all-reduce | flops 2 | bytes 16 | tf_op jit(solution)/shard_map/psum | solution.py:112
  538.1 18.5 %multiply_convert_fusion = bf16[32,16,64,256]{3,2,1,0:T(8,128)(2,1)} fusion(f32[32,16,64,256]{3,2,1,0:T(8,128)} %get-tuple-element.29, f32[]{:T(128)S(6)} %rsqrt.3, f32[]{:T(128)S(6)} %div.32), kind=kLoop, calls=%fused_computation.11 | loop fusion | flops 25165824 | bytes 50331656 | tf_op jit(solution)/shard_map/convert_element_type | solution.py:115
  (42 shorter events, 77.0 us)
Async XLA Ops:
  0.0 459.7 %copy-start = (bf16[64,64]{1,0:T(8,128)(2,1)S(1)}, bf16[64,64]{1,0:T(8,128)(2,1)}, u32[]{:S(2)}) copy-start(bf16[64,64]{1,0:T(8,128)(2,1)} %param.5) | copy-start | bytes 24580
  34.0 95.5 %all-to-all-start = ((bf16[4,2,262144]{2,1,0:T(2,128)(2,1)}), bf16[4,2,262144]{2,1,0:T(2,128)(2,1)}, u32[]{:S(2)}, u32[]{:S(2)}) async-start(bf16[4,2,262144]{2,1,0:T(2,128)(2,1)} %reshape.539), calls=%async_computation | async-start | bytes 8388608 | tf_op jit(solution)/shard_map/all_to_all | solution.py:79
  175.7 18.4 %all-to-all-start.1 = ((bf16[8,2,32768]{2,1,0:T(2,128)(2,1)}), bf16[8,2,32768]{2,1,0:T(2,128)(2,1)S(1)}, u32[]{:S(2)}, u32[]{:S(2)}) async-start(bf16[8,2,32768]{2,1,0:T(2,128)(2,1)} %reshape.541), calls=%async_computation.1 | async-start | bytes 2097152 | tf_op jit(solution)/shard_map/all_to_all | solution.py:85
  314.9 97.9 %all-to-all-start.3 = ((bf16[4,2,262144]{2,1,0:T(2,128)(2,1)}), bf16[4,2,262144]{2,1,0:T(2,128)(2,1)}, u32[]{:S(2)}, u32[]{:S(2)}) async-start(bf16[4,2,262144]{2,1,0:T(2,128)(2,1)} %reshape.545), calls=%async_computation.3 | async-start | bytes 8388608 | tf_op jit(solution)/shard_map/all_to_all | solution.py:102
